TPU v7x, 32 devices: a whole 2x2x4 slice. The times are simulated.
32 devices in a mesh: shard: 16 (over z, y, core), model: 2 (over x).
Axes of the slice: x: 2, y: 2, z: 4, core: 2. Of those that a mesh axis runs over, the one named last changes fastest.
Arguments:
- gradients: float32 [128, 128, 4096], P(None, 'shard', 'model'), may hold values from -6 to 6
- momentum: float32 [128, 128, 4096], P(None, 'shard', 'model'), may hold values from -6 to 6
- weights: float32 [128, 128, 4096], P(None, 'shard', 'model'), may hold values from -0.1875 to 0.1875
Outputs:
- new_weights: float32 [128, 128, 4096], P(None, 'shard', 'model')
- new_momentum: float32 [128, 128, 4096], P(None, 'shard', 'model')
All inputs are finite; a program needn't handle non-finite values.
Results may differ from a plain program's by a relative error of at most 0.0001.
Values sent between devices are 32-bit elements; how exact they have to be, the bound alone decides.
A program may use at most 128 MiB of HBM per device.

v0:
```python
import jax
import jax.numpy as jnp
from jax import lax
from jax.sharding import PartitionSpec as P

ITERS = 3


hold_rate = 0.9
learn_rate = 0.9
decay_rate = 0.1


def body(gradients, momentum, weights):
    new_momentum = hold_rate * momentum + gradients
    moved = lax.all_to_all(new_momentum, "shard", split_axis=0, concat_axis=1, tiled=True)
    total = lax.psum(jnp.sum(moved * moved, axis=(1, 2), keepdims=True), "model")
    iterate = moved * lax.rsqrt(total + 1e-06)
    for step in range(ITERS):
        gram = lax.psum(
            jnp.einsum("mik,mjk->mij", iterate, iterate, precision=lax.Precision.HIGHEST), "model"
        )
        mixed = -4.775 * gram + 2.0315 * jnp.einsum(
            "mij,mjk->mik", gram, gram, precision=lax.Precision.HIGHEST
        )
        iterate = 3.4445 * iterate + jnp.einsum(
            "mij,mjk->mik", mixed, iterate, precision=lax.Precision.HIGHEST
        )
    back = lax.all_to_all(iterate, "shard", split_axis=1, concat_axis=0, tiled=True)
    new_weights = (1.0 - learn_rate * decay_rate) * weights - learn_rate * back
    return (new_weights, new_momentum)


def solution(mesh):
    placed = (P(None, "shard", "model"), P(None, "shard", "model"), P(None, "shard", "model"))
    return jax.shard_map(
        body,
        mesh=mesh,
        in_specs=placed,
        out_specs=(P(None, "shard", "model"), P(None, "shard", "model")),
        check_vma=False,
    )
```

profile of v0, /device:TPU:1, one launch (start us, length us, event | category | flops | bytes accessed | tf_op | source)
XLA Modules:
  0.0 612.6 jit_solution(11765519909520166831)
XLA Ops:
  7.2 0.0 all-reduce.4.cloned.1.call-start
  7.2 12.0 %multiply_add_fusion.3 = f32[128,8,2048]{2,1,0:T(8,128)} fusion(f32[128,8,2048]{2,1,0:T(8,128)} %param.3, f32[128,8,2048]{2,1,0:T(8,128)} %param.4), kind=kLoop, calls=%fused_computation.7 | loop fusion | flops 4194304 | bytes 25165824 | tf_op jit(solution)/shard_map/add | solution.py:15
  19.2 189.9 %all_to_all.27 = f32[128,8,2048]{2,1,0:T(8,128)S(1)} all-to-all(f32[128,8,2048]{2,1,0:T(8,128)} %multiply_add_fusion.3), channel_id=1, replica_groups=mesh['shard'=16,'model'=2] {'shard'}, dimensions={0} | all-to-all | bytes 16777216 | tf_op jit(solution)/shard_map/all_to_all | solution.py:16
  209.1 0.0 copy-start
  209.1 3.4 copy-done
  212.5 0.8 fusion
  213.3 4.1 psum.28
  217.3 12.9 %fusion.2 = f32[8,128,128]{2,1,0:T(8,128)} fusion(f32[16,8,8,2048]{3,2,1,0:T(8,128)} %bitcast.38, f32[8]{0:T(128)S(1)} %rsqrt_bitcast_fusion), kind=kOutput, calls=%fused_computation.9 | convolution fusion | flops 3223322624 | bytes 8912928 | tf_op jit(solution)/shard_map/mik,mjk->mij/dot_general | solution.py:21
  230.2 0.0 all-reduce.4.cloned.1.call-update
  230.3 0.3 all-reduce.6.cloned.1.call-start
  230.6 29.0 %all-reduce.4.cloned.1.call-done = f32[8,128,128]{2,1,0:T(8,128)} async-done(((f32[8,128,128]{2,1,0:T(8,128)}), f32[8,128,128]{2,1,0:T(8,128)}) %all-reduce.4.cloned.1.call-update) | async-done | bytes 524304 | tf_op jit(solution)/shard_map/psum | solution.py:20
  259.6 2.1 fusion.7
  261.7 12.0 %multiply_add_fusion.2 = f32[8,128,2048]{2,1,0:T(8,128)S(1)} fusion(f32[16,8,8,2048]{3,2,1,0:T(8,128)} %bitcast.39, f32[8,128,128]{2,1,0:T(8,128)S(1)} %fusion.7, f32[8]{0:T(128)S(1)} %rsqrt_bitcast_fusion), kind=kOutput, calls=%fused_computation.6 | convolution fusion | flops 3229614080 | bytes 17301536 | tf_op jit(solution)/shard_map/mij,mjk->mik/dot_general | solution.py:26
  273.7 0.0 copy-start.1
  273.7 3.4 copy-done.1
  277.1 8.5 %fusion.8 = f32[8,128,128]{2,1,0:T(8,128)} fusion(f32[8,128,2048]{2,1,0:T(8,128)S(1)} %multiply_add_fusion.2), kind=kOutput, calls=%fused_computation.20 | convolution fusion | flops 3221225472 | bytes 8912896 | tf_op jit(solution)/shard_map/mik,mjk->mij/dot_general | solution.py:21
  285.7 0.0 all-reduce.6.cloned.1.call-update
  285.7 0.0 all-reduce.8.cloned.1.call-start
  285.7 28.8 %all-reduce.6.cloned.1.call-done = f32[8,128,128]{2,1,0:T(8,128)} async-done(((f32[8,128,128]{2,1,0:T(8,128)}), f32[8,128,128]{2,1,0:T(8,128)}) %all-reduce.6.cloned.1.call-update) | async-done | bytes 524304 | tf_op jit(solution)/shard_map/psum | solution.py:20
  314.5 2.1 fusion.6
  316.6 14.1 %multiply_add_fusion.1 = f32[8,128,2048]{2,1,0:T(8,128)S(1)} fusion(f32[8,128,2048]{2,1,0:T(8,128)} %copy-done.1, f32[8,128,128]{2,1,0:T(8,128)S(1)} %fusion.6), kind=kOutput, calls=%fused_computation.5 | convolution fusion | flops 3225419776 | bytes 17301504 | tf_op jit(solution)/shard_map/mij,mjk->mik/dot_general | solution.py:26
  330.6 0.0 copy-start.2
  330.7 3.4 copy-done.2
  334.0 8.5 %fusion.9 = f32[8,128,128]{2,1,0:T(8,128)} fusion(f32[8,128,2048]{2,1,0:T(8,128)S(1)} %multiply_add_fusion.1), kind=kOutput, calls=%fused_computation.21 | convolution fusion | flops 3221225472 | bytes 8912896 | tf_op jit(solution)/shard_map/mik,mjk->mij/dot_general | solution.py:21
  342.6 0.0 all-reduce.8.cloned.1.call-update
  342.6 28.8 %all-reduce.8.cloned.1.call-done = f32[8,128,128]{2,1,0:T(8,128)} async-done(((f32[8,128,128]{2,1,0:T(8,128)}), f32[8,128,128]{2,1,0:T(8,128)}) %all-reduce.8.cloned.1.call-update) | async-done | bytes 524304 | tf_op jit(solution)/shard_map/psum | solution.py:20
  371.4 2.1 fusion.5
  373.5 14.8 %multiply_add_fusion = f32[8,128,2048]{2,1,0:T(8,128)S(1)} fusion(f32[8,128,2048]{2,1,0:T(8,128)} %copy-done.2, f32[8,128,128]{2,1,0:T(8,128)S(1)} %fusion.5), kind=kOutput, calls=%fused_computation.4 | convolution fusion | flops 3225419776 | bytes 17301504 | tf_op jit(solution)/shard_map/mij,mjk->mik/dot_general | solution.py:26
  388.3 4.9 copy.8
  393.2 188.9 %all_to_all.28 = f32[8,128,2048]{2,0,1:T(8,128)S(1)} all-to-all(f32[8,128,2048]{2,0,1:T(8,128)S(1)} %copy.8), channel_id=1, replica_groups=mesh['shard'=16,'model'=2] {'shard'}, dimensions={1} | all-to-all | bytes 16777216 | tf_op jit(solution)/shard_map/all_to_all | solution.py:29
  582.1 1.8 broadcast_multiply_fusion
  583.9 9.7 %copy.9 = f32[16,8,8,2048]{3,2,1,0:T(8,128)} copy(f32[16,8,8,2048]{3,1,2,0:T(8,128)S(1)} %bitcast.40) | data formatting | bytes 16777216 | tf_op jit(solution)/shard_map/mul | solution.py:30
  593.6 12.0 %bitcast_subtract_fusion = f32[128,8,2048]{2,1,0:T(8,128)} fusion(f32[16,8,8,2048]{3,2,1,0:T(8,128)} %copy.9, f32[128,8,2048]{2,1,0:T(8,128)} %param.5), kind=kLoop, calls=%fused_computation.1 | loop fusion | flops 4194304 | bytes 25165824 | tf_op jit(solution)/shard_map/sub | solution.py:30
  (1 shorter events, 0.0 us)
Async XLA Ops:
  7.2 252.5 %all-reduce.4.cloned.1.call-start = ((), (), s32[]{:S(2)}) async-start(), calls=%async_computation.2 | async-start | bytes 1048576 | tf_op jit(solution)/shard_map/psum | solution.py:20
  209.1 3.4 copy-start
  230.3 84.2 %all-reduce.6.cloned.1.call-start = ((), (), s32[]{:S(2)}) async-start(), calls=%async_computation.3 | async-start | bytes 1048576 | tf_op jit(solution)/shard_map/psum | solution.py:20
  273.7 3.4 copy-start.1
  285.7 85.7 %all-reduce.8.cloned.1.call-start = ((), (), s32[]{:S(2)}) async-start(), calls=%async_computation.4 | async-start | bytes 1048576 | tf_op jit(solution)/shard_map/psum | solution.py:20
  330.6 3.4 copy-start.2
Sparse Core Ops, SparseCore 0:
  230.4 29.1 all-reduce.3
  285.8 28.6 all-reduce.5
  342.7 28.6 all-reduce.7
where the time goes:
time: 618 us; the launch traced here: 613 us
  blocking collectives  383 us (62%)
  waiting for transfers between devices  86.6 us (14%)
  matrix products  77.1 us (12%)
  other arithmetic  26.6 us (4%)
  local copies, waits for them, and re-layouts  24.7 us (4%)
  between operations  14.3 us (2%)
    all_to_all x1, blocking collectives, body(): lax.all_to_all(new_momentum, 'shard', split_axis=0, concat_axis=1, tiled=...  190 us
    all_to_all x1, blocking collectives, body(): lax.all_to_all(iterate, 'shard', split_axis=1, concat_axis=0, tiled=True)  189 us
    psum x3, waiting for transfers between devices, body(): lax.psum(jnp.einsum('mik,mjk->mij', iterate, iterate, precision=lax.Preci...  86.6 us
    dot_general x3, matrix products, body(): jnp.einsum('mij,mjk->mik', mixed, iterate, precision=lax.Precision.HIGHEST)  40.9 us
    dot_general x3, matrix products, body(): jnp.einsum('mik,mjk->mij', iterate, iterate, precision=lax.Precision.HIGH...  29.9 us
  transfers between devices with their start and end apart: 3, of which 3 were waited for; matrix products, arithmetic and copies ran while one was open for 0% of the time, Pallas kernels for 0%

commit v1 on v0

v1 whole, which is shorter than its diff:
```python
import functools

import jax
import jax.numpy as jnp
from jax import lax
from jax.experimental import pallas as pl
from jax.experimental.pallas import tpu as pltpu
from jax.sharding import PartitionSpec as P

ITERS = 3
AHEAD = 2

hold_rate = 0.9
learn_rate = 0.9
decay_rate = 0.1

MESH = pl.DeviceIdType.MESH


def dot(a, b, contract):
    return lax.dot_general(
        a,
        b,
        ((contract[0], contract[1]), ((), ())),
        precision=lax.Precision.HIGHEST,
        preferred_element_type=jnp.float32,
    )


def mul(a, b):
    return dot(a, b, ((1,), (0,)))


def mixer(gram, eye):
    total = jnp.sum(jnp.sum(gram * eye, axis=1, keepdims=True), axis=0, keepdims=True)
    scale = lax.rsqrt(total + 1e-06)
    a = gram * scale * scale
    q = None
    for step in range(ITERS):
        p = 3.4445 * eye + (-4.775 * a + 2.0315 * mul(a, a))
        q = p if q is None else mul(p, q)
        if step < ITERS - 1:
            a = mul(mul(p, a), p)
    return q * scale


def flipped(me, k, n):
    out, bit = 0, 1
    while bit < n:
        own = (me // bit) % 2
        out = out + bit * ((1 - own) if (k // bit) % 2 else own)
        bit *= 2
    return out


def exchange_kernel(n, models, moved_ref, back_ref, x, y, gram, peers, send1, recv1, send2, recv2, gsend, grecv):
    me = lax.axis_index("shard")
    col = lax.axis_index("model")
    mats, rows, cols = moved_ref.shape
    per = mats // n
    side = n * rows
    chunk = min(cols, 512)
    order = sorted(range(1, n), reverse=True)
    dests = [flipped(me, k, n) for k in order]
    mine = pl.ds(pl.multiple_of(me * rows, rows), rows)

    barrier = pltpu.get_barrier_semaphore()
    for dest in dests:
        pl.semaphore_signal(barrier, inc=1, device_id={"shard": dest}, device_id_type=MESH)
    for step in range(1, models):
        pl.semaphore_signal(barrier, inc=1, device_id={"model": (col + step) % models}, device_id_type=MESH)
    pl.semaphore_wait(barrier, n - 1 + models - 1)

    def forth(c):
        for dest in dests:
            pltpu.make_async_remote_copy(
                src_ref=moved_ref.at[dest * per + c],
                dst_ref=x.at[c, mine, :],
                send_sem=send1.at[c],
                recv_sem=recv1.at[c],
                device_id={"shard": dest},
                device_id_type=MESH,
            ).start()
        pltpu.make_async_copy(moved_ref.at[me * per + c], x.at[c, mine, :], recv1.at[c]).start()

    def back(c):
        for dest in dests:
            theirs = pl.ds(pl.multiple_of(dest * rows, rows), rows)
            pltpu.make_async_remote_copy(
                src_ref=y.at[c, theirs, :],
                dst_ref=back_ref.at[me * per + c],
                send_sem=send2.at[c],
                recv_sem=recv2,
                device_id={"shard": dest},
                device_id_type=MESH,
            ).start()
        pltpu.make_async_copy(y.at[c, mine, :], back_ref.at[me * per + c], recv2).start()

    for c in range(min(AHEAD, per)):
        forth(c)

    eye = (
        lax.broadcasted_iota(jnp.int32, (side, side), 0) == lax.broadcasted_iota(jnp.int32, (side, side), 1)
    ).astype(jnp.float32)

    def round_(c, carry):
        pltpu.make_async_copy(x.at[c], x.at[c], recv1.at[c]).wait()

        def part(k, total):
            piece = x[c, :, pl.ds(pl.multiple_of(k * chunk, chunk), chunk)]
            return total + dot(piece, piece, ((1,), (1,)))

        gram[c] = lax.fori_loop(0, cols // chunk, part, jnp.zeros((side, side), jnp.float32))

        @pl.when(c + AHEAD < per)
        def _():
            forth(c + AHEAD)

        copies = []
        for step in range(1, models):
            copy = pltpu.make_async_remote_copy(
                src_ref=gram.at[c],
                dst_ref=peers.at[step - 1, c],
                send_sem=gsend.at[step - 1, c],
                recv_sem=grecv.at[step - 1, c],
                device_id={"model": (col + step) % models},
                device_id_type=MESH,
            )
            copy.start()
            copies.append(copy)
        whole = gram[c]
        for step, copy in enumerate(copies):
            copy.wait()
            whole = whole + peers[step, c]
        q = mixer(whole, eye)

        def apply(k, carry):
            at = pl.ds(pl.multiple_of(k * chunk, chunk), chunk)
            y[c, :, at] = mul(q, x[c, :, at])
            return carry

        lax.fori_loop(0, cols // chunk, apply, 0)
        back(c)
        return carry

    lax.fori_loop(0, per, round_, 0)

    def drain(c, carry):
        sent = x.at[c, pl.ds(0, side - rows), :]
        pltpu.make_async_copy(sent, sent, send1.at[c]).wait()
        pltpu.make_async_copy(sent, sent, send2.at[c]).wait()
        return carry

    lax.fori_loop(0, per, drain, 0)
    pltpu.make_async_copy(back_ref, back_ref, recv2).wait()


def exchange(moved, n, models):
    mats, rows, cols = moved.shape
    per, side = mats // n, n * rows
    others = max(models - 1, 1)
    return pl.pallas_call(
        functools.partial(exchange_kernel, n, models),
        out_shape=jax.ShapeDtypeStruct(moved.shape, jnp.float32),
        in_specs=[pl.BlockSpec(memory_space=pl.ANY)],
        out_specs=pl.BlockSpec(memory_space=pl.ANY),
        scratch_shapes=[
            pltpu.VMEM((per, side, cols), jnp.float32),
            pltpu.VMEM((per, side, cols), jnp.float32),
            pltpu.VMEM((per, side, side), jnp.float32),
            pltpu.VMEM((others, per, side, side), jnp.float32),
            pltpu.SemaphoreType.DMA((per,)),
            pltpu.SemaphoreType.DMA((per,)),
            pltpu.SemaphoreType.DMA((per,)),
            pltpu.SemaphoreType.DMA,
            pltpu.SemaphoreType.DMA((others, per)),
            pltpu.SemaphoreType.DMA((others, per)),
        ],
        compiler_params=pltpu.CompilerParams(
            collective_id=0, has_side_effects=True, vmem_limit_bytes=48 * 1024 * 1024
        ),
    )(moved)


def exchange_plain(new_momentum):
    moved = lax.all_to_all(new_momentum, "shard", split_axis=0, concat_axis=1, tiled=True)
    gram = lax.psum(
        jnp.einsum("mik,mjk->mij", moved, moved, precision=lax.Precision.HIGHEST), "model"
    )
    eye = jnp.eye(gram.shape[-1], dtype=jnp.float32)
    q = jax.vmap(lambda g: mixer(g, eye))(gram)
    iterate = jnp.einsum("mij,mjk->mik", q, moved, precision=lax.Precision.HIGHEST)
    return lax.all_to_all(iterate, "shard", split_axis=1, concat_axis=0, tiled=True)


def body(n, models, gradients, momentum, weights):
    new_momentum = hold_rate * momentum + gradients
    mats, rows, cols = new_momentum.shape
    direct = n & (n - 1) == 0 and rows % 8 == 0 and cols % 128 == 0 and 2 * mats * rows * cols * 4 <= 32 << 20
    if direct:
        back = exchange(new_momentum, n, models)
    else:
        back = exchange_plain(new_momentum)
    new_weights = (1.0 - learn_rate * decay_rate) * weights - learn_rate * back
    return (new_weights, new_momentum)


def solution(mesh):
    placed = (P(None, "shard", "model"), P(None, "shard", "model"), P(None, "shard", "model"))
    return jax.shard_map(
        functools.partial(body, mesh.shape["shard"], mesh.shape["model"]),
        mesh=mesh,
        in_specs=placed,
        out_specs=(P(None, "shard", "model"), P(None, "shard", "model")),
        check_vma=False,
    )
```

time: 618 us -> 402 us (0.65)
  blocking collectives: 383 us -> 0 us
  Pallas kernels: 0 us -> 376 us
  waiting for transfers between devices: 86.6 us -> 0 us
  matrix products: 77.1 us -> 0 us
  local copies, waits for them, and re-layouts: 24.7 us -> 0 us
  between operations: 14.3 us -> 0.64 us
    all_to_all x2 -> x0, blocking collectives: 379 us -> none  [the longest x1 190 us: body(): lax.all_to_all(new_momentum, 'shard', split_axis=0, concat_axis=1, tiled=...]
    pallas_call x0 -> x1, Pallas kernels: none -> 376 us  [exchange(): pl.pallas_call(functools.partial(exchange_kernel, n, models), out_shape=j...]
    psum x3 -> x0, waiting for transfers between devices: 86.6 us -> none  [body(): lax.psum(jnp.einsum('mik,mjk->mij', iterate, iterate, precision=lax.Preci...]
    dot_general x9 -> x0, matrix products: 77.1 us -> none  [the longest x3 40.9 us: body(): jnp.einsum('mij,mjk->mik', mixed, iterate, precision=lax.Precision.HIGHEST)]
    unnamed x6 -> x0, local copies, waits for them, and re-layouts: 10.2 us -> none
    mul x1 -> x0, local copies, waits for them, and re-layouts: 9.71 us -> none  [body(): new_weights = (1.0 - learn_rate * decay_rate) * weights - learn_rate * back]
  transfers between devices with their start and end apart: 3 -> 0, of which waited for: 3 -> 0; matrix products, arithmetic and copies ran while one was open for 0% -> 0% of each run, Pallas kernels for 0% -> 0%
where the time goes in v1:
time: 402 us; the launch traced here: 401 us
  Pallas kernels  376 us (94%)
  other arithmetic  24.1 us (6%)
    pallas_call x1, Pallas kernels, exchange(): pl.pallas_call(functools.partial(exchange_kernel, n, models), out_shape=j...  376 us
    sub x1, other arithmetic, body(): new_weights = (1.0 - learn_rate * decay_rate) * weights - learn_rate * back  12.1 us
    add x1, other arithmetic, body(): new_momentum = hold_rate * momentum + gradients  12 us

profile of v1, /device:TPU:1, one launch (start us, length us, event | category | flops | bytes accessed | tf_op | source)
XLA Modules:
  0.0 400.9 jit_solution(383867757326800943)
XLA Ops:
  0.6 12.0 %multiply_add_fusion.moved_ref = f32[128,8,2048]{2,1,0:T(8,128)} fusion(f32[128,8,2048]{2,1,0:T(8,128)} %param.3, f32[128,8,2048]{2,1,0:T(8,128)} %param.4), kind=kLoop, calls=%fused_computation.1 | loop fusion | flops 4194304 | bytes 25165824 | tf_op jit(solution)/shard_map/add | solution.py:197
  12.6 376.2 %shard_map.50 = f32[128,8,2048]{2,1,0:T(8,128)} custom-call(f32[128,8,2048]{2,1,0:T(8,128)} %multiply_add_fusion.moved_ref), custom_call_target="tpu_custom_call" | custom-call | tf_op jit(solution)/shard_map/pallas_call | solution.py:162
  388.8 12.1 %multiply_subtract_fusion = f32[128,8,2048]{2,1,0:T(8,128)} fusion(f32[128,8,2048]{2,1,0:T(8,128)} %shard_map.50, f32[128,8,2048]{2,1,0:T(8,128)} %param.5), kind=kLoop, calls=%fused_computation | loop fusion | flops 6291456 | bytes 25165824 | tf_op jit(solution)/shard_map/sub | solution.py:204

commit v2 on v1

--- a/solution.py
+++ b/solution.py
@@ -9,6 +9,7 @@
 
 ITERS = 3
 AHEAD = 2
+BEHIND = 3
 
 hold_rate = 0.9
 learn_rate = 0.9
@@ -53,50 +54,97 @@
     return out
 
 
-def exchange_kernel(n, models, moved_ref, back_ref, x, y, gram, peers, send1, recv1, send2, recv2, gsend, grecv):
+def step_kernel(
+    n, models, grad_ref, mom_ref, weight_ref, out_ref, new_ref,
+    x, gs, ms, ws, gram, peers, gload, mload, wload, send1, recv1, send2, recv2, gsend, grecv,
+):
     me = lax.axis_index("shard")
     col = lax.axis_index("model")
-    mats, rows, cols = moved_ref.shape
-    per = mats // n
+    _, per, rows, cols = grad_ref.shape
     side = n * rows
     chunk = min(cols, 512)
-    order = sorted(range(1, n), reverse=True)
-    dests = [flipped(me, k, n) for k in order]
+    dests = [flipped(me, k, n) for k in range(1, n)]
     mine = pl.ds(pl.multiple_of(me * rows, rows), rows)
 
-    barrier = pltpu.get_barrier_semaphore()
-    for dest in dests:
-        pl.semaphore_signal(barrier, inc=1, device_id={"shard": dest}, device_id_type=MESH)
-    for step in range(1, models):
-        pl.semaphore_signal(barrier, inc=1, device_id={"model": (col + step) % models}, device_id_type=MESH)
-    pl.semaphore_wait(barrier, n - 1 + models - 1)
+    def loads(c):
+        slot = c % 2
+        return (
+            pltpu.make_async_copy(grad_ref.at[:, c], gs.at[slot], gload.at[slot]),
+            pltpu.make_async_copy(mom_ref.at[:, c], ms.at[slot], mload.at[slot]),
+        )
+
+    def weight_load(c):
+        slot = c % 2
+        return pltpu.make_async_copy(weight_ref.at[:, c], ws.at[slot], wload.at[slot])
+
+    def load(c):
+        for copy in loads(c):
+            copy.start()
+
+    def make(c):
+        for copy in loads(c):
+            copy.wait()
+        slot = c % 2
+
+        def one(j, carry):
+            new_ref[j, c] = hold_rate * ms[slot, j] + gs[slot, j]
+            return carry
+
+        lax.fori_loop(0, n, one, 0)
+
+    def finish(c):
+        got = out_ref.at[:, c]
+        pltpu.make_async_copy(got, got, recv2.at[c]).wait()
+        weight_load(c).wait()
+        slot = c % 2
+
+        def one(j, carry):
+            out_ref[j, c] = (1.0 - learn_rate * decay_rate) * ws[slot, j] - learn_rate * out_ref[j, c]
+            return carry
+
+        lax.fori_loop(0, n, one, 0)
 
     def forth(c):
         for dest in dests:
             pltpu.make_async_remote_copy(
-                src_ref=moved_ref.at[dest * per + c],
+                src_ref=new_ref.at[dest, c],
                 dst_ref=x.at[c, mine, :],
                 send_sem=send1.at[c],
                 recv_sem=recv1.at[c],
                 device_id={"shard": dest},
                 device_id_type=MESH,
             ).start()
-        pltpu.make_async_copy(moved_ref.at[me * per + c], x.at[c, mine, :], recv1.at[c]).start()
+        pltpu.make_async_copy(new_ref.at[me, c], x.at[c, mine, :], recv1.at[c]).start()
 
     def back(c):
         for dest in dests:
             theirs = pl.ds(pl.multiple_of(dest * rows, rows), rows)
             pltpu.make_async_remote_copy(
-                src_ref=y.at[c, theirs, :],
-                dst_ref=back_ref.at[me * per + c],
+                src_ref=x.at[c, theirs, :],
+                dst_ref=out_ref.at[me, c],
                 send_sem=send2.at[c],
-                recv_sem=recv2,
+                recv_sem=recv2.at[c],
                 device_id={"shard": dest},
                 device_id_type=MESH,
             ).start()
-        pltpu.make_async_copy(y.at[c, mine, :], back_ref.at[me * per + c], recv2).start()
-
-    for c in range(min(AHEAD, per)):
+        pltpu.make_async_copy(x.at[c, mine, :], out_ref.at[me, c], recv2.at[c]).start()
+
+    barrier = pltpu.get_barrier_semaphore()
+    for dest in dests:
+        pl.semaphore_signal(barrier, inc=1, device_id={"shard": dest}, device_id_type=MESH)
+    for step in range(1, models):
+        pl.semaphore_signal(barrier, inc=1, device_id={"model": (col + step) % models}, device_id_type=MESH)
+    for c in range(min(2, per)):
+        load(c)
+        weight_load(c).start()
+    make(0)
+    pl.semaphore_wait(barrier, n - 1 + models - 1)
+    forth(0)
+    for c in range(2, min(AHEAD + 2, per + 1)):
+        if c < per:
+            load(c)
+        make(c - 1)
+    for c in range(1, min(AHEAD, per)):
         forth(c)
 
     eye = (
@@ -136,11 +184,29 @@
 
         def apply(k, carry):
             at = pl.ds(pl.multiple_of(k * chunk, chunk), chunk)
-            y[c, :, at] = mul(q, x[c, :, at])
+            x[c, :, at] = mul(q, x[c, :, at])
             return carry
 
         lax.fori_loop(0, cols // chunk, apply, 0)
+
+        @pl.when(c + AHEAD + 1 < per)
+        def _():
+            make(c + AHEAD + 1)
+
+        @pl.when(c + AHEAD + 2 < per)
+        def _():
+            load(c + AHEAD + 2)
+
         back(c)
+
+        @pl.when(c >= BEHIND)
+        def _():
+            finish(c - BEHIND)
+
+            @pl.when(c - BEHIND + 2 < per)
+            def _():
+                weight_load(c - BEHIND + 2).start()
+
         return carry
 
     lax.fori_loop(0, per, round_, 0)
@@ -148,38 +214,62 @@
     def drain(c, carry):
         sent = x.at[c, pl.ds(0, side - rows), :]
         pltpu.make_async_copy(sent, sent, send1.at[c]).wait()
+        return carry
+
+    lax.fori_loop(0, per, drain, 0)
+
+    def last(c, carry):
+        finish(c)
+
+        @pl.when(c + 2 < per)
+        def _():
+            weight_load(c + 2).start()
+
+        return carry
+
+    lax.fori_loop(max(per - BEHIND, 0), per, last, 0)
+
+    def drain_back(c, carry):
+        sent = x.at[c, pl.ds(0, side - rows), :]
         pltpu.make_async_copy(sent, sent, send2.at[c]).wait()
         return carry
 
-    lax.fori_loop(0, per, drain, 0)
-    pltpu.make_async_copy(back_ref, back_ref, recv2).wait()
-
-
-def exchange(moved, n, models):
-    mats, rows, cols = moved.shape
+    lax.fori_loop(0, per, drain_back, 0)
+
+
+def step_direct(gradients, momentum, weights, n, models):
+    mats, rows, cols = gradients.shape
     per, side = mats // n, n * rows
     others = max(models - 1, 1)
-    return pl.pallas_call(
-        functools.partial(exchange_kernel, n, models),
-        out_shape=jax.ShapeDtypeStruct(moved.shape, jnp.float32),
-        in_specs=[pl.BlockSpec(memory_space=pl.ANY)],
-        out_specs=pl.BlockSpec(memory_space=pl.ANY),
+    split = (n, per, rows, cols)
+    placed = pltpu.VMEM(split, jnp.float32)
+    out, new = pl.pallas_call(
+        functools.partial(step_kernel, n, models),
+        out_shape=(placed, placed),
+        in_specs=[pl.BlockSpec(memory_space=pltpu.HBM)] * 3,
+        out_specs=[pl.BlockSpec(memory_space=pltpu.VMEM)] * 2,
         scratch_shapes=[
             pltpu.VMEM((per, side, cols), jnp.float32),
-            pltpu.VMEM((per, side, cols), jnp.float32),
+            pltpu.VMEM((2, n, rows, cols), jnp.float32),
+            pltpu.VMEM((2, n, rows, cols), jnp.float32),
+            pltpu.VMEM((2, n, rows, cols), jnp.float32),
             pltpu.VMEM((per, side, side), jnp.float32),
             pltpu.VMEM((others, per, side, side), jnp.float32),
+            pltpu.SemaphoreType.DMA((2,)),
+            pltpu.SemaphoreType.DMA((2,)),
+            pltpu.SemaphoreType.DMA((2,)),
             pltpu.SemaphoreType.DMA((per,)),
             pltpu.SemaphoreType.DMA((per,)),
             pltpu.SemaphoreType.DMA((per,)),
-            pltpu.SemaphoreType.DMA,
+            pltpu.SemaphoreType.DMA((per,)),
             pltpu.SemaphoreType.DMA((others, per)),
             pltpu.SemaphoreType.DMA((others, per)),
         ],
         compiler_params=pltpu.CompilerParams(
-            collective_id=0, has_side_effects=True, vmem_limit_bytes=48 * 1024 * 1024
+            collective_id=0, has_side_effects=True, vmem_limit_bytes=40 * 1024 * 1024
         ),
-    )(moved)
+    )(*(array.reshape(split) for array in (gradients, momentum, weights)))
+    return out.reshape(gradients.shape), new.reshape(gradients.shape)
 
 
 def exchange_plain(new_momentum):
@@ -194,13 +284,12 @@
 
 
 def body(n, models, gradients, momentum, weights):
+    mats, rows, cols = gradients.shape
+    size = mats * rows * cols * 4
+    if n & (n - 1) == 0 and rows % 8 == 0 and cols % 128 == 0 and size <= 8 << 20 and mats // n > BEHIND:
+        return step_direct(gradients, momentum, weights, n, models)
     new_momentum = hold_rate * momentum + gradients
-    mats, rows, cols = new_momentum.shape
-    direct = n & (n - 1) == 0 and rows % 8 == 0 and cols % 128 == 0 and 2 * mats * rows * cols * 4 <= 32 << 20
-    if direct:
-        back = exchange(new_momentum, n, models)
-    else:
-        back = exchange_plain(new_momentum)
+    back = exchange_plain(new_momentum)
     new_weights = (1.0 - learn_rate * decay_rate) * weights - learn_rate * back
     return (new_weights, new_momentum)
 

time: 402 us -> 377 us (0.938)
  other arithmetic: 24.1 us -> 0 us
  Pallas kernels: 376 us -> 365 us
  local copies, waits for them, and re-layouts: 0 us -> 6.8 us
    sub x1 -> x0, other arithmetic: 12.1 us -> none  [body(): new_weights = (1.0 - learn_rate * decay_rate) * weights - learn_rate * back]
    add x1 -> x0, other arithmetic: 12 us -> none  [body(): new_momentum = hold_rate * momentum + gradients]
    pallas_call x1, Pallas kernels: 376 us -> 365 us  [step_direct(): pl.pallas_call(functools.partial(step_kernel, n, models), out_shape=(plac...]
    unnamed x0 -> x2, local copies, waits for them, and re-layouts: none -> 6.8 us
where the time goes in v2:
time: 377 us; the launch traced here: 372 us
  Pallas kernels  365 us (97%)
  local copies, waits for them, and re-layouts  6.8 us (2%)
    pallas_call x1, Pallas kernels, step_direct(): pl.pallas_call(functools.partial(step_kernel, n, models), out_shape=(plac...  365 us

profile of v2, /device:TPU:1, one launch (start us, length us, event | category | flops | bytes accessed | tf_op | source)
XLA Modules:
  0.0 372.0 jit_solution(1770476323068181512)
XLA Ops:
  0.6 364.6 %shard_map.50 = (f32[16,8,8,2048]{3,2,1,0:T(8,128)S(1)}, f32[16,8,8,2048]{3,2,1,0:T(8,128)S(1)}) custom-call(f32[16,8,8,2048]{3,2,1,0:T(8,128)} %bitcast.7, f32[16,8,8,2048]{3,2,1,0:T(8,128)} %bitcast.8, f32[16,8,8,2048]{3,2,1,0:T(8,128)} %bitcast.9), custom_call_target="tpu_custom_call" | custom-call | tf_op jit(solution)/shard_map/pallas_call | solution.py:246
  365.2 3.4 copy.7
  368.6 3.4 copy.8
